TPU v7x, 32 devices: a whole 2x2x4 slice. The times are simulated.
32 devices in a mesh: rows: 8 (over z, y), cols: 4 (over x, core).
Axes of the slice: x: 2, y: 2, z: 4, core: 2. Of those that a mesh axis runs over, the one named last changes fastest.
Arguments:
- tile_values: bfloat16 [8, 4, 320, 128, 128], P('rows', 'cols'), may hold values from -0.0625 to 0.0625
- tile_rows: int32 [8, 4, 320], P('rows', 'cols'), may hold values from 0 to 7
- tile_cols: int32 [8, 4, 320], P('rows', 'cols'), may hold values from 0 to 15
- tile_counts: int32 [8, 4], P('rows', 'cols'), may hold values from 1 to 320, as said below
- sketch: bfloat16 [8192, 160], P(('rows', 'cols')), may hold values from -6 to 6
Outputs:
- basis: float32 [8192, 160], P(('rows', 'cols'))
- factor: float32 [160, 160], replicated
Inputs may be any that keep to these rules, and one draw needn't show every extreme that they name: Only the first tile_counts[r, c] slots of list (r, c) are live; some list has all 320 slots live in every draw. `tile_cols`: the same place may stand in several live slots of a list.
All inputs are finite; a program needn't handle non-finite values.
Results may differ from a plain program's by a relative error of at most 0.0029.
Values may be sent and summed in bfloat16 or wider, within the bound.
A program may use at most 128 MiB of HBM per device.

v0:
```python
import math

import jax
import jax.numpy as jnp
from jax import lax
from jax.sharding import PartitionSpec as P

POWER = 2
RT = 8


def accumulate(block_list, row_list, col_list, live_count, gathered, height):
    slot_total = block_list.shape[0]
    tile_size = block_list.shape[1]
    sketch_width = gathered.shape[1]
    tile_stack = gathered.reshape(-1, tile_size, sketch_width)
    block_size = math.gcd(32, slot_total)

    def one_block(block_index, running):
        first_slot = block_index * block_size
        block_values = lax.dynamic_slice_in_dim(block_list, first_slot, block_size, 0)
        rowids = lax.dynamic_slice_in_dim(row_list, first_slot, block_size, 0)
        colids = lax.dynamic_slice_in_dim(col_list, first_slot, block_size, 0)
        picked = jnp.take(tile_stack, colids, axis=0)
        products = jnp.einsum(
            "sab,sbk->sak", block_values, picked, preferred_element_type=jnp.float32
        )
        live_mask = (first_slot + jnp.arange(block_size, dtype=jnp.int32) < live_count).astype(
            jnp.float32
        )
        return running.at[rowids].add(products * live_mask[:, None, None])

    block_count = (live_count + block_size - 1) // block_size
    initial = jnp.zeros((height, tile_size, sketch_width), jnp.float32)
    running = lax.fori_loop(0, block_count, one_block, initial)
    return running.reshape(height * tile_size, sketch_width)


def shards(tile_values, tile_rows, tile_cols, tile_counts, sketch):
    own_values = tile_values[0, 0]
    own_rows = tile_rows[0, 0]
    own_cols = tile_cols[0, 0]
    own_count = tile_counts[0, 0]
    nodes_total = sketch.shape[0] * lax.axis_size("rows") * lax.axis_size("cols")
    current = sketch
    solved = None
    factor = None
    for power in range(POWER):
        gathered = lax.all_gather(current, "rows", axis=0, tiled=True)
        partial_value = accumulate(own_values, own_rows, own_cols, own_count, gathered, RT)
        whole = lax.psum(partial_value, "cols")
        gram_matrix = lax.psum(jnp.dot(whole.T, whole, precision=lax.Precision.HIGHEST), "rows")
        share_rows = whole.shape[0] // lax.axis_size("cols")
        owned = lax.dynamic_slice_in_dim(whole, lax.axis_index("cols") * share_rows, share_rows, 0)
        gram_matrix = gram_matrix / nodes_total
        factor = jnp.linalg.cholesky(gram_matrix)
        solved = lax.linalg.triangular_solve(
            factor, owned, left_side=False, lower=True, transpose_a=True
        )
        current = solved.astype(jnp.bfloat16)
    return (solved, factor)


def solution(mesh):
    placed = (
        P("rows", "cols", None, None, None),
        P("rows", "cols", None),
        P("rows", "cols", None),
        P("rows", "cols"),
        P(("rows", "cols"), None),
    )
    return jax.shard_map(
        shards,
        mesh=mesh,
        in_specs=placed,
        out_specs=(P(("rows", "cols"), None), P()),
        check_vma=False,
    )
```

profile of v0, /device:TPU:0, one launch (start us, length us, event | category | flops | bytes accessed | tf_op | source)
XLA Modules:
  0.0 599.5 jit_solution(8288383398452547619)
XLA Ops:
  9.3 33.6 %all_gather.6 = bf16[2048,160]{0,1:T(8,128)(2,1)S(1)} all-gather(bf16[256,160]{0,1:T(8,128)(2,1)} %param.18), channel_id=1, replica_groups=mesh['rows'=8,'cols'=4] {'rows'}, dimensions={0}, use_global_device_ids=true | all-gather | bytes 737280 | tf_op jit(solution)/shard_map/all_gather | solution.py:49
  44.2 59.3 %while.23 = (s32[]{:T(128)}, f32[8,128,160]{1,2,0:T(8,128)S(1)}, s32[]{:T(128)}, s32[320]{0:T(512)S(1)}, bf16[320,128,128]{2,1,0:T(8,128)(2,1)}, /*index=5*/s32[...) while((s32[]{:T(128)}, f32[8,128,160]{1,2,0:T(8,128)S(1)}, ...), condition=%wide.region_2.4_spmd, body=%wide.region_0.3_spmd.sunk | while | flops 169739648 | bytes 16258423 | solution.py:35
  45.0 3.3 gather_fusion
  54.9 3.3 gather_fusion
  74.6 3.3 gather_fusion
  84.5 3.3 gather_fusion
  94.4 3.3 gather_fusion
  104.6 72.0 %all-reduce.8.cloned.1.call-done = f32[1024,160]{0,1:T(8,128)} async-done(((f32[1024,160]{0,1:T(8,128)}), f32[1024,160]{0,1:T(8,128)}) %all-reduce.8.cloned.1.call-update) | async-done | bytes 655376 | tf_op jit(solution)/shard_map/psum | solution.py:51
  179.5 71.0 %all-reduce.10.cloned.1.call-done = f32[160,160]{0,1:T(8,128)} async-done(((f32[160,160]{0,1:T(8,128)}), f32[160,160]{0,1:T(8,128)}) %all-reduce.10.cloned.1.call-update) | async-done | bytes 102416 | tf_op jit(solution)/shard_map/psum | solution.py:52
  252.5 11.7 %cholesky.136 = f32[128,128]{1,0:T(8,128)S(1)} custom-call(f32[128,128]{1,0:T(8,128)S(1)} %cholesky.208), custom_call_target="Cholesky" | custom-call | tf_op jit(solution)/shard_map/jit(cholesky)/cholesky | solution.py:56
  264.3 9.8 %custom-call.13 = f32[1,128,128]{1,2,0:T(8,128)S(1)} custom-call(f32[1,128,128]{2,1,0:T(8,128)S(1)} %get-tuple-element.178), custom_call_target="InvertDiagBlocksLowerTriangular" | custom-call | tf_op jit(solution)/shard_map/jit(cholesky)/cholesky | solution.py:56
  280.1 19.7 %custom-call.14 = f32[2,128,128]{1,2,0:T(8,128)S(1)} custom-call(f32[2,128,128]{2,1,0:T(8,128)S(1)} %pad_maximum_fusion.1), custom_call_target="InvertDiagBlocksLowerTriangular" | custom-call | tf_op jit(solution)/shard_map/triangular_solve/custom-call.0 | solution.py:57
  302.2 32.0 %all_gather.7 = bf16[2048,160]{0,1:T(8,128)(2,1)S(1)} all-gather(bf16[256,160]{0,1:T(8,128)(2,1)S(1)} %maximum_convert_fusion), channel_id=1, replica_groups=mesh['rows'=8,'cols'=4] {'rows'}, dimensions={0}, use_global_device_ids=true | all-gather | bytes 737280 | tf_op jit(solution)/shard_map/all_gather | solution.py:49
  335.6 59.3 %while.24 = (s32[]{:T(128)}, f32[8,128,160]{1,2,0:T(8,128)S(1)}, s32[]{:T(128)}, s32[320]{0:T(512)S(1)}, bf16[320,128,128]{2,1,0:T(8,128)(2,1)}, /*index=5*/s32[...) while((s32[]{:T(128)}, f32[8,128,160]{1,2,0:T(8,128)S(1)}, ...), condition=%wide.region_11.15_spmd, body=%wide.region_9.14_spmd.sunk | while | flops 169739648 | bytes 16258423 | solution.py:35
  336.3 3.3 gather_fusion.1
  356.1 3.3 gather_fusion.1
  366.0 3.3 gather_fusion.1
  375.9 3.3 gather_fusion.1
  385.8 3.3 gather_fusion.1
  396.1 70.0 %all-reduce.12.cloned.1.call-done = f32[1024,160]{0,1:T(8,128)} async-done(((f32[1024,160]{0,1:T(8,128)}), f32[1024,160]{0,1:T(8,128)}) %all-reduce.12.cloned.1.call-update) | async-done | bytes 655376 | tf_op jit(solution)/shard_map/psum | solution.py:51
  468.8 71.1 %all-reduce.14.cloned.1.call-done = f32[160,160]{0,1:T(8,128)} async-done(((f32[160,160]{0,1:T(8,128)}), f32[160,160]{0,1:T(8,128)}) %all-reduce.14.cloned.1.call-update) | async-done | bytes 102416 | tf_op jit(solution)/shard_map/psum | solution.py:52
  542.0 11.7 %cholesky.174 = f32[128,128]{1,0:T(8,128)S(1)} custom-call(f32[128,128]{1,0:T(8,128)S(1)} %cholesky.211), custom_call_target="Cholesky" | custom-call | tf_op jit(solution)/shard_map/jit(cholesky)/cholesky | solution.py:56
  553.7 9.8 %custom-call.15 = f32[1,128,128]{1,2,0:T(8,128)S(1)} custom-call(f32[1,128,128]{2,1,0:T(8,128)S(1)} %get-tuple-element.176), custom_call_target="InvertDiagBlocksLowerTriangular" | custom-call | tf_op jit(solution)/shard_map/jit(cholesky)/cholesky | solution.py:56
  570.2 19.7 %custom-call.16 = f32[2,128,128]{1,2,0:T(8,128)S(1)} custom-call(f32[2,128,128]{2,1,0:T(8,128)S(1)} %pad_maximum_fusion.2), custom_call_target="InvertDiagBlocksLowerTriangular" | custom-call | tf_op jit(solution)/shard_map/triangular_solve/custom-call.0 | solution.py:57
  (123 shorter events, 116.9 us)
Async XLA Ops:
  7.2 169.4 %all-reduce.8.cloned.1.call-start = ((), (), s32[]{:S(2)}) async-start(), calls=%async_computation | async-start | bytes 1310720 | tf_op jit(solution)/shard_map/psum | solution.py:51
  104.5 146.0 %all-reduce.10.cloned.1.call-start = ((), (), s32[]{:S(2)}) async-start(), calls=%async_computation.1 | async-start | bytes 327680 | tf_op jit(solution)/shard_map/psum | solution.py:52
  179.2 286.9 %all-reduce.12.cloned.1.call-start = ((), (), s32[]{:S(2)}) async-start(), calls=%async_computation.2 | async-start | bytes 1310720 | tf_op jit(solution)/shard_map/psum | solution.py:51
  395.8 144.1 %all-reduce.14.cloned.1.call-start = ((), (), s32[]{:S(2)}) async-start(), calls=%async_computation.3 | async-start | bytes 327680 | tf_op jit(solution)/shard_map/psum | solution.py:52
Sparse Core Ops, SparseCore 0:
  104.6 71.9 all-reduce.7
  180.5 70.0 all-reduce.9
  396.0 70.1 all-reduce.11
  469.9 70.0 all-reduce.13
where the time goes:
time: 600 us
  waiting for transfers between devices  284 us (47%)
  other arithmetic  143 us (24%)
  blocking collectives  65.7 us (11%)
  matrix products  44.3 us (7%)
  local copies, waits for them, and re-layouts  43.9 us (7%)
  between operations  17.3 us (3%)
    psum x2, waiting for transfers between devices, shards(): lax.psum(jnp.dot(whole.T, whole, precision=lax.Precision.HIGHEST), 'rows')  142 us
    psum x2, waiting for transfers between devices, shards(): whole = lax.psum(partial_value, 'cols')  142 us
    all_gather x2, blocking collectives, shards(): gathered = lax.all_gather(current, 'rows', axis=0, tiled=True)  65.7 us
    another operation x14, other arithmetic, shards(): factor = jnp.linalg.cholesky(gram_matrix)  51.6 us
    another operation x11, other arithmetic, shards(): lax.linalg.triangular_solve(factor, owned, left_side=False, lower=True, t...  40.9 us
    gather x12, local copies, waits for them, and re-layouts, one_block(): picked = jnp.take(tile_stack, colids, axis=0)  39.1 us
    scatter-add x12, other arithmetic, one_block(): return running.at[rowids].add(products * live_mask[:, None, None])  35.6 us
    dot_general x12, matrix products, one_block(): jnp.einsum('sab,sbk->sak', block_values, picked, preferred_element_type=j...  33.6 us
  transfers between devices with their start and end apart: 4, of which 4 were waited for; matrix products, arithmetic and copies ran while one was open for 0% of the time, Pallas kernels for 0%

commit v1 on v0

--- a/solution.py
+++ b/solution.py
@@ -1,12 +1,322 @@
+import functools
 import math
 
 import jax
 import jax.numpy as jnp
 from jax import lax
+from jax.experimental import pallas as pl
+from jax.experimental.pallas import tpu as pltpu
 from jax.sharding import PartitionSpec as P
 
 POWER = 2
 RT = 8
+LANES = 128
+BLOCK = 32
+VMEM_BYTES = 60 * 1024 * 1024
+MESH = pl.DeviceIdType.MESH
+HIGHEST = lax.Precision.HIGHEST
+NT = (((1,), (1,)), ((), ()))
+TN = (((0,), (0,)), ((), ()))
+
+
+def densify_kernel(height, pair, rows_ref, cols_ref, count_ref, tiles_ref, high_ref, low_ref, head, size, following):
+    groups = high_ref.shape[0]
+    tile = tiles_ref.shape[1]
+    places = groups * pair * height
+
+    def clear(place, _):
+        head[place] = 0
+        size[place] = 0
+        return 0
+
+    def link(slot, _):
+        place = cols_ref[slot] * height + rows_ref[slot]
+        following[slot] = head[place]
+        head[place] = slot
+        size[place] = size[place] + 1
+        return 0
+
+    lax.fori_loop(0, places, clear, 0)
+    lax.fori_loop(0, count_ref[0], link, 0)
+
+    def one_place(index, _):
+        group = index // height
+        row = index % height
+        for part in range(pair):
+            place = (group * pair + part) * height + row
+
+            def add(_, carry):
+                slot, total = carry
+                return following[slot], total + tiles_ref[slot].astype(jnp.float32)
+
+            start = (head[place], jnp.zeros((tile, tile), jnp.float32))
+            _, total = lax.fori_loop(0, size[place], add, start)
+            high = total.astype(jnp.bfloat16)
+            low = (total - high.astype(jnp.float32)).astype(jnp.bfloat16)
+            where = pl.ds(pl.multiple_of(row * tile, tile), tile)
+            high_ref[group, where, part * tile:(part + 1) * tile] = high
+            low_ref[group, where, part * tile:(part + 1) * tile] = low
+        return 0
+
+    lax.fori_loop(0, groups * height, one_place, 0)
+
+
+def densify(tile_values, tile_rows, tile_cols, tile_counts, groups, pair):
+    slots, tile = tile_values.shape[:2]
+    places = groups * pair * RT
+    smem = pl.BlockSpec(memory_space=pltpu.SMEM)
+    vmem = pl.BlockSpec(memory_space=pltpu.VMEM)
+    dense = jax.ShapeDtypeStruct((groups, RT * tile, pair * tile), jnp.bfloat16)
+    return pl.pallas_call(
+        functools.partial(densify_kernel, RT, pair),
+        out_shape=(dense, dense),
+        in_specs=[smem, smem, smem, vmem],
+        out_specs=(vmem, vmem),
+        scratch_shapes=[
+            pltpu.SMEM((places,), jnp.int32),
+            pltpu.SMEM((places,), jnp.int32),
+            pltpu.SMEM((slots,), jnp.int32),
+        ],
+        compiler_params=pltpu.CompilerParams(vmem_limit_bytes=VMEM_BYTES),
+        name="densify",
+    )(tile_rows, tile_cols, tile_counts, tile_values)
+
+
+def image_kernel(
+    n_rows, n_cols, current_ref, high_ref, low_ref, image_ref, gram_ref,
+    gathered, part, came, packed, gram_cols, gram_rows, gram_whole,
+    own_send, own_recv, pass_send, pass_recv, part_send, part_recv,
+    gc_send, gc_recv, gr_send, gr_recv, gw_send, gw_recv,
+):
+    row = lax.axis_index("rows")
+    col = lax.axis_index("cols")
+    width, share = current_ref.shape
+    deep = n_rows // 2
+    z = row // 2
+    y = row % 2
+    mate = z * 2 + 1 - y
+
+    def send(src, dst, send_sem, recv_sem, **where):
+        return pltpu.make_async_remote_copy(
+            src_ref=src, dst_ref=dst, send_sem=send_sem, recv_sem=recv_sem,
+            device_id=where, device_id_type=MESH,
+        )
+
+    barrier = pltpu.get_barrier_semaphore()
+    for step in range(1, n_rows):
+        pl.semaphore_signal(barrier, inc=1, device_id={"rows": (row + step) % n_rows}, device_id_type=MESH)
+    for step in range(1, n_cols):
+        pl.semaphore_signal(barrier, inc=1, device_id={"cols": (col + step) % n_cols}, device_id_type=MESH)
+    pl.semaphore_wait(barrier, n_rows + n_cols - 2)
+
+    sent = []
+    own = send(current_ref, gathered.at[row], pass_send.at[z], pass_recv.at[z], rows=mate)
+    own.start()
+    sent.append(own)
+    for step in range(1, deep):
+        to = ((z + step) % deep) * 2 + y
+        copy = send(current_ref, gathered.at[row], own_send.at[step], own_recv.at[z], rows=to)
+        copy.start()
+        sent.append(copy)
+
+    def multiply(value, source, first):
+        for piece in range(n_cols):
+            high = high_ref[source, piece * share:(piece + 1) * share, :]
+            low = low_ref[source, piece * share:(piece + 1) * share, :]
+            got = lax.dot_general(value, high, NT, preferred_element_type=jnp.float32)
+            got = got + lax.dot_general(value, low, NT, preferred_element_type=jnp.float32)
+            part[piece] = got if first else part[piece] + got
+
+    multiply(current_ref[...], row, True)
+    for step in range(1, deep):
+        other = (z + step) % deep
+        source = other * 2 + y
+        send(current_ref, gathered.at[source], own_send.at[step], own_recv.at[other], rows=mate).wait_recv()
+        copy = send(gathered.at[source], gathered.at[source], pass_send.at[other], pass_recv.at[other], rows=mate)
+        copy.start()
+        sent.append(copy)
+        multiply(gathered[source], source, False)
+    for step in range(deep):
+        other = (z + step) % deep
+        source = other * 2 + 1 - y
+        send(current_ref, gathered.at[source], pass_send.at[other], pass_recv.at[other], rows=mate).wait_recv()
+        multiply(gathered[source], source, False)
+    for copy in sent:
+        copy.wait_send()
+
+    twin = col + 1 - 2 * (col % 2)
+    across = (col + 2) % 4
+    twin_across = (twin + 2) % 4
+    first = send(part.at[twin_across], came.at[1], part_send.at[1], part_recv.at[1], cols=twin)
+    second = send(part.at[twin], came.at[0], part_send.at[0], part_recv.at[0], cols=twin)
+    first.start()
+    second.start()
+    first.wait()
+    came[3] = part[across] + came[1]
+    third = send(came.at[3], came.at[2], part_send.at[2], part_recv.at[2], cols=across)
+    third.start()
+    second.wait()
+    near = part[col] + came[0]
+    third.wait()
+    image = near + came[2]
+    image_ref[...] = image
+
+    gram = lax.dot_general(image, image, NT, precision=HIGHEST, preferred_element_type=jnp.float32)
+    rest = width - LANES
+    packed[0:width, :] = gram[:, 0:LANES]
+    packed[width:width + rest, :] = jnp.zeros((rest, LANES), jnp.float32)
+    packed[width:width + rest, 0:rest] = gram[LANES:width, LANES:width]
+    piece_rows = (width + rest) // n_cols
+    copies = []
+    for step in range(1, n_cols):
+        to = (col + step) % n_cols
+        src = packed.at[pl.ds(pl.multiple_of(to * piece_rows, 8), piece_rows)]
+        copy = send(src, gram_cols.at[col], gc_send.at[step], gc_recv.at[col], cols=to)
+        copy.start()
+        copies.append(copy)
+    gram_cols[col] = packed[pl.ds(pl.multiple_of(col * piece_rows, 8), piece_rows), :]
+    for step in range(1, n_cols):
+        source = (col + step) % n_cols
+        send(packed.at[pl.ds(0, piece_rows)], gram_cols.at[source], gc_send.at[step], gc_recv.at[source], cols=source).wait_recv()
+    total = gram_cols[0]
+    for piece in range(1, n_cols):
+        total = total + gram_cols[piece]
+    gram_rows[row] = total
+    for step in range(1, n_rows):
+        to = (row + step) % n_rows
+        copy = send(gram_rows.at[row], gram_rows.at[row], gr_send.at[step], gr_recv.at[row], rows=to)
+        copy.start()
+        copies.append(copy)
+    for step in range(1, n_rows):
+        source = (row + step) % n_rows
+        send(gram_rows.at[source], gram_rows.at[source], gr_send.at[step], gr_recv.at[source], rows=source).wait_recv()
+    total = gram_rows[0]
+    for piece in range(1, n_rows):
+        total = total + gram_rows[piece]
+    gram_whole[col] = total
+    for step in range(1, n_cols):
+        to = (col + step) % n_cols
+        copy = send(gram_whole.at[col], gram_whole.at[col], gw_send.at[step], gw_recv.at[col], cols=to)
+        copy.start()
+        copies.append(copy)
+    for step in range(1, n_cols):
+        source = (col + step) % n_cols
+        send(gram_whole.at[source], gram_whole.at[source], gw_send.at[step], gw_recv.at[source], cols=source).wait_recv()
+    for piece in range(n_cols):
+        gram_ref[piece * piece_rows:(piece + 1) * piece_rows, :] = gram_whole[piece]
+    for copy in copies:
+        copy.wait_send()
+
+
+def image_step(n_rows, n_cols, current, high, low):
+    width, share = current.shape
+    lines = 2 * width - LANES
+    piece = lines // n_cols
+    vmem = pl.BlockSpec(memory_space=pltpu.VMEM)
+    dma = pltpu.SemaphoreType.DMA
+    f32 = jnp.float32
+    return pl.pallas_call(
+        functools.partial(image_kernel, n_rows, n_cols),
+        out_shape=(jax.ShapeDtypeStruct((width, share), f32), jax.ShapeDtypeStruct((lines, LANES), f32)),
+        in_specs=[vmem, vmem, vmem],
+        out_specs=(vmem, vmem),
+        scratch_shapes=[
+            pltpu.VMEM((n_rows, width, share), jnp.bfloat16),
+            pltpu.VMEM((n_cols, width, share), f32),
+            pltpu.VMEM((4, width, share), f32),
+            pltpu.VMEM((lines, LANES), f32),
+            pltpu.VMEM((n_cols, piece, LANES), f32),
+            pltpu.VMEM((n_rows, piece, LANES), f32),
+            pltpu.VMEM((n_cols, piece, LANES), f32),
+            dma((n_rows // 2,)), dma((n_rows // 2,)), dma((n_rows // 2,)), dma((n_rows // 2,)),
+            dma((3,)), dma((3,)),
+            dma((n_cols,)), dma((n_cols,)), dma((n_rows,)), dma((n_rows,)), dma((n_cols,)), dma((n_cols,)),
+        ],
+        compiler_params=pltpu.CompilerParams(
+            collective_id=0, has_side_effects=True, vmem_limit_bytes=VMEM_BYTES
+        ),
+        name="image_step",
+    )(current, high, low)
+
+
+def solve_kernel(nodes, packed_ref, image_ref, solved_ref, rounded_ref, upper_ref, work):
+    width = image_ref.shape[0]
+    rest = width - LANES
+    half = work.shape[1] // 2
+    work[...] = jnp.zeros_like(work)
+    work[:, 0:LANES] = packed_ref[0:width, :] / nodes
+    work[0:LANES, LANES:width] = (packed_ref[LANES:width, :] / nodes).T
+    work[LANES:width, LANES:width] = packed_ref[width:width + rest, 0:rest] / nodes
+    row_ids = lax.broadcasted_iota(jnp.int32, (width, half), 0)
+    col_ids = lax.broadcasted_iota(jnp.int32, (width, half), 1)
+    work[:, half:] = (row_ids == col_ids).astype(jnp.float32)
+    r_ids = lax.broadcasted_iota(jnp.int32, (BLOCK, BLOCK), 0)
+    c_ids = lax.broadcasted_iota(jnp.int32, (BLOCK, BLOCK), 1)
+    eye = r_ids == c_ids
+    lines = lax.broadcasted_iota(jnp.int32, (BLOCK, 1), 0)
+    for first in range(0, width, BLOCK):
+        last = first + BLOCK
+        diag = work[first:last, first:last]
+        inverse = eye.astype(jnp.float32)
+        for j in range(BLOCK):
+            scale = jnp.where(lines > j, diag[:, j:j + 1] / diag[j:j + 1, j:j + 1], 0.0)
+            inverse = inverse - scale * inverse[j:j + 1, :]
+            diag = diag - scale * diag[j:j + 1, :]
+        pivots = jnp.sum(jnp.where(eye, diag, 0.0), axis=1, keepdims=True)
+        inverse = inverse / jnp.sqrt(pivots)
+        panel = jnp.dot(inverse, work[first:last, :], precision=HIGHEST, preferred_element_type=jnp.float32)
+        work[first:last, :] = panel
+        if last < width:
+            drop = lax.dot_general(panel[:, last:width], panel, TN, precision=HIGHEST, preferred_element_type=jnp.float32)
+            work[last:width, :] = work[last:width, :] - drop
+    upper_ref[...] = jnp.where(col_ids >= row_ids, work[:, 0:half], 0.0)[:, 0:width]
+    solved = jnp.dot(work[:, half:half + width], image_ref[...], precision=HIGHEST, preferred_element_type=jnp.float32)
+    solved_ref[...] = solved
+    rounded_ref[...] = solved.astype(jnp.bfloat16)
+
+
+def solve_step(nodes, packed, image):
+    width, share = image.shape
+    vmem = pl.BlockSpec(memory_space=pltpu.VMEM)
+    return pl.pallas_call(
+        functools.partial(solve_kernel, nodes),
+        out_shape=(
+            jax.ShapeDtypeStruct((width, share), jnp.float32),
+            jax.ShapeDtypeStruct((width, share), jnp.bfloat16),
+            jax.ShapeDtypeStruct((width, width), jnp.float32),
+        ),
+        in_specs=[vmem, vmem],
+        out_specs=(vmem, vmem, vmem),
+        scratch_shapes=[pltpu.VMEM((width, 4 * LANES), jnp.float32)],
+        compiler_params=pltpu.CompilerParams(vmem_limit_bytes=VMEM_BYTES),
+        name="solve_step",
+    )(packed, image)
+
+
+def dense_shards(n_rows, n_cols, tile_values, tile_rows, tile_cols, tile_counts, sketch):
+    tile = tile_values.shape[-1]
+    pair = sketch.shape[0] // tile
+    high, low = densify(tile_values[0, 0], tile_rows[0, 0], tile_cols[0, 0], tile_counts[0], n_rows, pair)
+    current = sketch.T
+    nodes = float(sketch.shape[0] * n_rows * n_cols)
+    for power in range(POWER):
+        image, packed = image_step(n_rows, n_cols, current, high, low)
+        solved, current, upper = solve_step(nodes, packed, image)
+    return (solved.T, upper.T)
+
+
+def fits_dense(mesh, tile_values, sketch):
+    n_rows, n_cols = mesh.shape["rows"], mesh.shape["cols"]
+    tile = tile_values.shape[-1]
+    share = sketch.shape[0] // (n_rows * n_cols)
+    width = sketch.shape[1]
+    dense = n_rows * share * RT * tile * 2
+    lists = tile_values.shape[2] * tile * tile * 2
+    return (
+        n_cols == 4 and n_rows % 2 == 0 and tile == LANES and share % tile == 0
+        and RT * tile == n_cols * share and LANES < width <= 2 * LANES and width % BLOCK == 0
+        and (2 * width - LANES) % (8 * n_cols) == 0 and 2 * dense + lists < 40 * 1024 * 1024
+    )
 
 
 def accumulate(block_list, row_list, col_list, live_count, gathered, height):
@@ -69,10 +379,17 @@
         P("rows", "cols"),
         P(("rows", "cols"), None),
     )
-    return jax.shard_map(
-        shards,
-        mesh=mesh,
-        in_specs=placed,
-        out_specs=(P(("rows", "cols"), None), P()),
-        check_vma=False,
-    )
+
+    def run(*arrays):
+        body = shards
+        if fits_dense(mesh, arrays[0], arrays[4]):
+            body = functools.partial(dense_shards, mesh.shape["rows"], mesh.shape["cols"])
+        return jax.shard_map(
+            body,
+            mesh=mesh,
+            in_specs=placed,
+            out_specs=(P(("rows", "cols"), None), P()),
+            check_vma=False,
+        )(*arrays)
+
+    return run

time: 600 us -> 141 us (0.23)
  waiting for transfers between devices: 284 us -> 0 us
  other arithmetic: 143 us -> 2.55 us
  Pallas kernels: 0 us -> 135 us
  blocking collectives: 65.7 us -> 0 us
  matrix products: 44.3 us -> 0 us
  local copies, waits for them, and re-layouts: 43.9 us -> 1.69 us
  between operations: 17.3 us -> 1.3 us
    psum x4 -> x0, waiting for transfers between devices: 284 us -> none  [the longest x2 142 us: shards(): lax.psum(jnp.dot(whole.T, whole, precision=lax.Precision.HIGHEST), 'rows')]
    pallas_call x0 -> x5, Pallas kernels: none -> 135 us  [the longest x2 84.9 us: image_step(): pl.pallas_call(functools.partial(image_kernel, n_rows, n_cols), out_shape...]
    another operation x25 -> x0, other arithmetic: 92.5 us -> none  [the longest x14 51.6 us: shards(): factor = jnp.linalg.cholesky(gram_matrix)]
    all_gather x2 -> x0, blocking collectives: 65.7 us -> none  [shards(): gathered = lax.all_gather(current, 'rows', axis=0, tiled=True)]
    gather x12 -> x0, local copies, waits for them, and re-layouts: 39.1 us -> none  [one_block(): picked = jnp.take(tile_stack, colids, axis=0)]
    dot_general x14 -> x0, matrix products: 38.9 us -> none  [the longest x12 33.6 us: one_block(): jnp.einsum('sab,sbk->sak', block_values, picked, preferred_element_type=j...]
    scatter-add x12 -> x0, other arithmetic: 35.6 us -> none  [one_block(): return running.at[rowids].add(products * live_mask[:, None, None])]
    and x12 -> x0, other arithmetic: 8.73 us -> none  [one_block(): picked = jnp.take(tile_stack, colids, axis=0)]
  transfers between devices with their start and end apart: 4 -> 0, of which waited for: 4 -> 0; matrix products, arithmetic and copies ran while one was open for 0% -> 0% of each run, Pallas kernels for 0% -> 0%
where the time goes in v1:
time: 141 us; the launch traced here: 140 us
  Pallas kernels  135 us (96%)
  other arithmetic  2.55 us (2%)
  local copies, waits for them, and re-layouts  1.69 us (1%)
    pallas_call x2, Pallas kernels, image_step(): pl.pallas_call(functools.partial(image_kernel, n_rows, n_cols), out_shape...  84.9 us
    pallas_call x2, Pallas kernels, solve_step(): pl.pallas_call(functools.partial(solve_kernel, nodes), out_shape=(jax.Sha...  35.3 us
    pallas_call x1, Pallas kernels, densify(): pl.pallas_call(functools.partial(densify_kernel, RT, pair), out_shape=(de...  14.7 us

profile of v1, /device:TPU:0, one launch (start us, length us, event | category | flops | bytes accessed | tf_op | source)
XLA Modules:
  0.0 140.4 jit_solution(5892705169558304159)
XLA Ops:
  1.3 1.3 reduce.rows_ref
  2.6 1.3 reduce.1.cols_ref
  3.8 14.7 %densify.1 = (bf16[8,1024,256]{2,1,0:T(8,128)(2,1)}, bf16[8,1024,256]{2,1,0:T(8,128)(2,1)}) custom-call(s32[320]{0:T(512)} %reduce.rows_ref, s32[320]{0:T(512)} %reduce.1.cols_ref, s32[1]{0:T(128)} %bitcast.5.count_ref, bf16[320,128,128]{2,1,0:T(8,128)(2,1)} %bitcast.6), custom_call_target="tpu_custom_call" | custom-call | tf_op jit(solution)/shard_map/densify/pallas_call | solution.py:70
  18.5 44.7 %image_step.2 = (f32[160,256]{1,0:T(8,128)}, f32[192,128]{1,0:T(8,128)}) custom-call(bf16[160,256]{1,0:T(8,128)(2,1)} %bitcast.8, bf16[8,1024,256]{2,1,0:T(8,128)(2,1)} %get-tuple-element.11.high_ref, bf16[8,1024,256]{2,1,0:T(8,128)(2,1)} %get-tuple-element.12.low_ref), custom_call_target="tpu_custom_call" | custom-call | tf_op jit(solution)/shard_map/image_step/pallas_call | solution.py:218
  63.2 17.6 %solve_step.2 = (f32[160,256]{1,0:T(8,128)}, bf16[160,256]{1,0:T(8,128)(2,1)}, f32[160,160]{1,0:T(8,128)}) custom-call(f32[192,128]{1,0:T(8,128)} %get-tuple-element.13.packed_ref, f32[160,256]{1,0:T(8,128)} %get-tuple-element.14.image_ref), custom_call_target="tpu_custom_call" | custom-call | tf_op jit(solution)/shard_map/solve_step/pallas_call | solution.py:281
  80.8 40.2 %image_step.3 = (f32[160,256]{1,0:T(8,128)}, f32[192,128]{1,0:T(8,128)}) custom-call(bf16[160,256]{1,0:T(8,128)(2,1)} %get-tuple-element.15.current_ref, bf16[8,1024,256]{2,1,0:T(8,128)(2,1)} %get-tuple-element.11.high_ref, bf16[8,1024,256]{2,1,0:T(8,128)(2,1)} %get-tuple-element.12.low_ref), custom_call_target="tpu_custom_call" | custom-call | tf_op jit(solution)/shard_map/image_step/pallas_call | solution.py:218
  121.1 17.6 %solve_step.3 = (f32[160,256]{1,0:T(8,128)}, bf16[160,256]{1,0:T(8,128)(2,1)}, f32[160,160]{1,0:T(8,128)}) custom-call(f32[192,128]{1,0:T(8,128)} %get-tuple-element.16.packed_ref, f32[160,256]{1,0:T(8,128)} %get-tuple-element.17.image_ref), custom_call_target="tpu_custom_call" | custom-call | tf_op jit(solution)/shard_map/solve_step/pallas_call | solution.py:281
  138.7 1.7 %copy.7 = f32[160,160]{1,0:T(8,128)} copy(f32[160,160]{0,1:T(8,128)} %bitcast.7) | data formatting | bytes 204800

commit v2 on v1

--- a/solution.py
+++ b/solution.py
@@ -19,10 +19,15 @@
 TN = (((0,), (0,)), ((), ()))
 
 
-def densify_kernel(height, pair, rows_ref, cols_ref, count_ref, tiles_ref, high_ref, low_ref, head, size, following):
+def densify_kernel(
+    height, pair, rows_ref, cols_ref, count_ref, values_ref, high_ref, low_ref,
+    tiles_ref, head, size, following, loaded,
+):
     groups = high_ref.shape[0]
     tile = tiles_ref.shape[1]
     places = groups * pair * height
+    load = pltpu.make_async_copy(values_ref, tiles_ref, loaded)
+    load.start()
 
     def clear(place, _):
         head[place] = 0
@@ -30,14 +35,15 @@
         return 0
 
     def link(slot, _):
-        place = cols_ref[slot] * height + rows_ref[slot]
+        place = cols_ref[0, 0, slot] * height + rows_ref[0, 0, slot]
         following[slot] = head[place]
         head[place] = slot
         size[place] = size[place] + 1
         return 0
 
     lax.fori_loop(0, places, clear, 0)
-    lax.fori_loop(0, count_ref[0], link, 0)
+    lax.fori_loop(0, count_ref[0, 0], link, 0)
+    load.wait()
 
     def one_place(index, _):
         group = index // height
@@ -70,12 +76,14 @@
     return pl.pallas_call(
         functools.partial(densify_kernel, RT, pair),
         out_shape=(dense, dense),
-        in_specs=[smem, smem, smem, vmem],
+        in_specs=[smem, smem, smem, pl.BlockSpec(memory_space=pl.ANY)],
         out_specs=(vmem, vmem),
         scratch_shapes=[
+            pltpu.VMEM(tile_values.shape, tile_values.dtype),
             pltpu.SMEM((places,), jnp.int32),
             pltpu.SMEM((places,), jnp.int32),
             pltpu.SMEM((slots,), jnp.int32),
+            pltpu.SemaphoreType.DMA,
         ],
         compiler_params=pltpu.CompilerParams(vmem_limit_bytes=VMEM_BYTES),
         name="densify",
@@ -83,8 +91,8 @@
 
 
 def image_kernel(
-    n_rows, n_cols, current_ref, high_ref, low_ref, image_ref, gram_ref,
-    gathered, part, came, packed, gram_cols, gram_rows, gram_whole,
+    n_rows, n_cols, current_ref, high_hbm, low_hbm, image_ref, gram_ref,
+    high_ref, low_ref, loaded, gathered, part, came, packed, gram_cols, gram_rows, gram_whole,
     own_send, own_recv, pass_send, pass_recv, part_send, part_recv,
     gc_send, gc_recv, gr_send, gr_recv, gw_send, gw_recv,
 ):
@@ -102,6 +110,12 @@
             device_id=where, device_id_type=MESH,
         )
 
+    loads = [
+        pltpu.make_async_copy(high_hbm, high_ref, loaded.at[0]),
+        pltpu.make_async_copy(low_hbm, low_ref, loaded.at[1]),
+    ]
+    for load in loads:
+        load.start()
     barrier = pltpu.get_barrier_semaphore()
     for step in range(1, n_rows):
         pl.semaphore_signal(barrier, inc=1, device_id={"rows": (row + step) % n_rows}, device_id_type=MESH)
@@ -127,6 +141,8 @@
             got = got + lax.dot_general(value, low, NT, preferred_element_type=jnp.float32)
             part[piece] = got if first else part[piece] + got
 
+    for load in loads:
+        load.wait()
     multiply(current_ref[...], row, True)
     for step in range(1, deep):
         other = (z + step) % deep
@@ -218,9 +234,12 @@
     return pl.pallas_call(
         functools.partial(image_kernel, n_rows, n_cols),
         out_shape=(jax.ShapeDtypeStruct((width, share), f32), jax.ShapeDtypeStruct((lines, LANES), f32)),
-        in_specs=[vmem, vmem, vmem],
+        in_specs=[vmem, pl.BlockSpec(memory_space=pl.ANY), pl.BlockSpec(memory_space=pl.ANY)],
         out_specs=(vmem, vmem),
         scratch_shapes=[
+            pltpu.VMEM(high.shape, high.dtype),
+            pltpu.VMEM(low.shape, low.dtype),
+            dma((2,)),
             pltpu.VMEM((n_rows, width, share), jnp.bfloat16),
             pltpu.VMEM((n_cols, width, share), f32),
             pltpu.VMEM((4, width, share), f32),
@@ -239,7 +258,7 @@
     )(current, high, low)
 
 
-def solve_kernel(nodes, packed_ref, image_ref, solved_ref, rounded_ref, upper_ref, work):
+def solve_kernel(nodes, packed_ref, image_ref, solved_ref, rounded_ref, factor_ref, work):
     width = image_ref.shape[0]
     rest = width - LANES
     half = work.shape[1] // 2
@@ -258,10 +277,22 @@
         last = first + BLOCK
         diag = work[first:last, first:last]
         inverse = eye.astype(jnp.float32)
-        for j in range(BLOCK):
-            scale = jnp.where(lines > j, diag[:, j:j + 1] / diag[j:j + 1, j:j + 1], 0.0)
-            inverse = inverse - scale * inverse[j:j + 1, :]
-            diag = diag - scale * diag[j:j + 1, :]
+        for j in range(0, BLOCK, 2):
+            one = jnp.broadcast_to(diag[:, j:j + 1], (BLOCK, BLOCK))
+            two = jnp.broadcast_to(diag[:, j + 1:j + 2], (BLOCK, BLOCK))
+            a, b, c = one[j:j + 1, :], one[j + 1:j + 2, :], two[j + 1:j + 2, :]
+            u, v = diag[j:j + 1, :], diag[j + 1:j + 2, :]
+            s, t = inverse[j:j + 1, :], inverse[j + 1:j + 2, :]
+            slope = b * (1.0 / a)
+            below = lines > j + 1
+            left = jnp.where(below, one, 0.0)
+            right = jnp.where(below, two, 0.0) - left * slope
+            v_low, t_low = v - slope * u, t - slope * s
+            first_scale, second_scale = 1.0 / a, 1.0 / (c - slope * b)
+            diag = diag - left * (u * first_scale) - right * (v_low * second_scale)
+            inverse = inverse - left * (s * first_scale) - right * (t_low * second_scale)
+            diag = jnp.where(lines == j + 1, v_low, diag)
+            inverse = jnp.where(lines == j + 1, t_low, inverse)
         pivots = jnp.sum(jnp.where(eye, diag, 0.0), axis=1, keepdims=True)
         inverse = inverse / jnp.sqrt(pivots)
         panel = jnp.dot(inverse, work[first:last, :], precision=HIGHEST, preferred_element_type=jnp.float32)
@@ -269,7 +300,8 @@
         if last < width:
             drop = lax.dot_general(panel[:, last:width], panel, TN, precision=HIGHEST, preferred_element_type=jnp.float32)
             work[last:width, :] = work[last:width, :] - drop
-    upper_ref[...] = jnp.where(col_ids >= row_ids, work[:, 0:half], 0.0)[:, 0:width]
+    factor = jnp.where(col_ids >= row_ids, work[:, 0:half], 0.0).T
+    factor_ref[...] = factor[0:width, :]
     solved = jnp.dot(work[:, half:half + width], image_ref[...], precision=HIGHEST, preferred_element_type=jnp.float32)
     solved_ref[...] = solved
     rounded_ref[...] = solved.astype(jnp.bfloat16)
@@ -296,13 +328,13 @@
 def dense_shards(n_rows, n_cols, tile_values, tile_rows, tile_cols, tile_counts, sketch):
     tile = tile_values.shape[-1]
     pair = sketch.shape[0] // tile
-    high, low = densify(tile_values[0, 0], tile_rows[0, 0], tile_cols[0, 0], tile_counts[0], n_rows, pair)
+    high, low = densify(tile_values[0, 0], tile_rows, tile_cols, tile_counts, n_rows, pair)
     current = sketch.T
     nodes = float(sketch.shape[0] * n_rows * n_cols)
     for power in range(POWER):
         image, packed = image_step(n_rows, n_cols, current, high, low)
-        solved, current, upper = solve_step(nodes, packed, image)
-    return (solved.T, upper.T)
+        solved, current, factor = solve_step(nodes, packed, image)
+    return (solved.T, factor)
 
 
 def fits_dense(mesh, tile_values, sketch):

time: 141 us -> 137 us (0.972)
  other arithmetic: 2.55 us -> 0 us
  local copies, waits for them, and re-layouts: 1.69 us -> 0 us
    pallas_call x2, Pallas kernels: 35.3 us -> 44.1 us  [solve_step(): pl.pallas_call(functools.partial(solve_kernel, nodes), out_shape=(jax.Sha...]
    pallas_call x2, Pallas kernels: 84.9 us -> 79.7 us  [image_step(): pl.pallas_call(functools.partial(image_kernel, n_rows, n_cols), out_shape...]
    pallas_call x1, Pallas kernels: 14.7 us -> 11 us  [densify(): pl.pallas_call(functools.partial(densify_kernel, RT, pair), out_shape=(de...]
    unnamed x2 -> x0, other arithmetic: 2.55 us -> none
    unnamed x1 -> x0, local copies, waits for them, and re-layouts: 1.69 us -> none
where the time goes in v2:
time: 137 us; the launch traced here: 136 us
  Pallas kernels  135 us (99%)
    pallas_call x2, Pallas kernels, image_step(): pl.pallas_call(functools.partial(image_kernel, n_rows, n_cols), out_shape...  79.7 us
    pallas_call x2, Pallas kernels, solve_step(): pl.pallas_call(functools.partial(solve_kernel, nodes), out_shape=(jax.Sha...  44.1 us
    pallas_call x1, Pallas kernels, densify(): pl.pallas_call(functools.partial(densify_kernel, RT, pair), out_shape=(de...  11 us

profile of v2, /device:TPU:0, one launch (start us, length us, event | category | flops | bytes accessed | tf_op | source)
XLA Modules:
  0.0 136.2 jit_solution(16691640811069668239)
XLA Ops:
  1.3 11.0 %densify.1 = (bf16[8,1024,256]{2,1,0:T(8,128)(2,1)}, bf16[8,1024,256]{2,1,0:T(8,128)(2,1)}) custom-call(s32[1,1,320]{2,1,0:T(1,128)} %rows_ref.1, s32[1,1,320]{2,1,0:T(1,128)} %cols_ref.1, s32[1,1]{1,0:T(1,128)S(6)} %copy.7.count_ref, bf16[320,128,128]{2,1,0:T(8,128)(2,1)} %bitcast.3), custom_call_target="tpu_custom_call" | custom-call | tf_op jit(solution)/shard_map/densify/pallas_call | solution.py:76
  12.3 41.1 %image_step.2 = (f32[160,256]{1,0:T(8,128)}, f32[192,128]{1,0:T(8,128)}) custom-call(bf16[160,256]{1,0:T(8,128)(2,1)} %bitcast.4, bf16[8,1024,256]{2,1,0:T(8,128)(2,1)} %get-tuple-element.11.high_hbm, bf16[8,1024,256]{2,1,0:T(8,128)(2,1)} %get-tuple-element.12.low_hbm), custom_call_target="tpu_custom_call" | custom-call | tf_op jit(solution)/shard_map/image_step/pallas_call | solution.py:234
  53.4 22.1 %solve_step.2 = (f32[160,256]{1,0:T(8,128)}, bf16[160,256]{1,0:T(8,128)(2,1)}, f32[160,160]{1,0:T(8,128)}) custom-call(f32[192,128]{1,0:T(8,128)} %get-tuple-element.13.packed_ref, f32[160,256]{1,0:T(8,128)} %get-tuple-element.14.image_ref), custom_call_target="tpu_custom_call" | custom-call | tf_op jit(solution)/shard_map/solve_step/pallas_call | solution.py:313
  75.5 38.6 %image_step.3 = (f32[160,256]{1,0:T(8,128)}, f32[192,128]{1,0:T(8,128)}) custom-call(bf16[160,256]{1,0:T(8,128)(2,1)} %get-tuple-element.15.current_ref, bf16[8,1024,256]{2,1,0:T(8,128)(2,1)} %get-tuple-element.11.high_hbm, bf16[8,1024,256]{2,1,0:T(8,128)(2,1)} %get-tuple-element.12.low_hbm), custom_call_target="tpu_custom_call" | custom-call | tf_op jit(solution)/shard_map/image_step/pallas_call | solution.py:234
  114.1 22.1 %solve_step.3 = (f32[160,256]{1,0:T(8,128)}, bf16[160,256]{1,0:T(8,128)(2,1)}, f32[160,160]{1,0:T(8,128)}) custom-call(f32[192,128]{1,0:T(8,128)} %get-tuple-element.16.packed_ref, f32[160,256]{1,0:T(8,128)} %get-tuple-element.17.image_ref), custom_call_target="tpu_custom_call" | custom-call | tf_op jit(solution)/shard_map/solve_step/pallas_call | solution.py:313

commit v3 on v2

--- a/solution.py
+++ b/solution.py
@@ -269,32 +269,24 @@
     row_ids = lax.broadcasted_iota(jnp.int32, (width, half), 0)
     col_ids = lax.broadcasted_iota(jnp.int32, (width, half), 1)
     work[:, half:] = (row_ids == col_ids).astype(jnp.float32)
-    r_ids = lax.broadcasted_iota(jnp.int32, (BLOCK, BLOCK), 0)
-    c_ids = lax.broadcasted_iota(jnp.int32, (BLOCK, BLOCK), 1)
-    eye = r_ids == c_ids
-    lines = lax.broadcasted_iota(jnp.int32, (BLOCK, 1), 0)
+    r_ids = lax.broadcasted_iota(jnp.int32, (BLOCK, LANES), 0)
+    c_ids = lax.broadcasted_iota(jnp.int32, (BLOCK, LANES), 1)
+    start = (r_ids == c_ids).astype(jnp.float32)
+    lines = r_ids
     for first in range(0, width, BLOCK):
         last = first + BLOCK
         diag = work[first:last, first:last]
-        inverse = eye.astype(jnp.float32)
-        for j in range(0, BLOCK, 2):
-            one = jnp.broadcast_to(diag[:, j:j + 1], (BLOCK, BLOCK))
-            two = jnp.broadcast_to(diag[:, j + 1:j + 2], (BLOCK, BLOCK))
-            a, b, c = one[j:j + 1, :], one[j + 1:j + 2, :], two[j + 1:j + 2, :]
-            u, v = diag[j:j + 1, :], diag[j + 1:j + 2, :]
-            s, t = inverse[j:j + 1, :], inverse[j + 1:j + 2, :]
-            slope = b * (1.0 / a)
-            below = lines > j + 1
-            left = jnp.where(below, one, 0.0)
-            right = jnp.where(below, two, 0.0) - left * slope
-            v_low, t_low = v - slope * u, t - slope * s
-            first_scale, second_scale = 1.0 / a, 1.0 / (c - slope * b)
-            diag = diag - left * (u * first_scale) - right * (v_low * second_scale)
-            inverse = inverse - left * (s * first_scale) - right * (t_low * second_scale)
-            diag = jnp.where(lines == j + 1, v_low, diag)
-            inverse = jnp.where(lines == j + 1, t_low, inverse)
-        pivots = jnp.sum(jnp.where(eye, diag, 0.0), axis=1, keepdims=True)
-        inverse = inverse / jnp.sqrt(pivots)
+        columns = [jnp.broadcast_to(diag[:, k:k + 1], (BLOCK, LANES)) for k in range(BLOCK)]
+        inverse = start
+        for j in range(BLOCK):
+            scale = jnp.where(lines > j, columns[j] * (1.0 / columns[j][j:j + 1, :]), 0.0)
+            for k in range(j + 1, BLOCK):
+                columns[k] = columns[k] - scale * columns[k][j:j + 1, :]
+            inverse = inverse - scale * inverse[j:j + 1, :]
+        pivots = columns[0]
+        for k in range(1, BLOCK):
+            pivots = jnp.where(lines == k, columns[k], pivots)
+        inverse = (inverse / jnp.sqrt(pivots))[:, 0:BLOCK]
         panel = jnp.dot(inverse, work[first:last, :], precision=HIGHEST, preferred_element_type=jnp.float32)
         work[first:last, :] = panel
         if last < width:

time: 137 us -> 110 us (0.80)
  Pallas kernels: 135 us -> 109 us
    pallas_call x2, Pallas kernels: 44.1 us -> 16.4 us  [solve_step(): pl.pallas_call(functools.partial(solve_kernel, nodes), out_shape=(jax.Sha...]
    pallas_call x1, Pallas kernels: 11 us -> 13.5 us  [densify(): pl.pallas_call(functools.partial(densify_kernel, RT, pair), out_shape=(de...]
where the time goes in v3:
time: 110 us
  Pallas kernels  109 us (99%)
  between operations  1.3 us (1%)
    pallas_call x2, Pallas kernels, image_step(): pl.pallas_call(functools.partial(image_kernel, n_rows, n_cols), out_shape...  78.8 us
    pallas_call x2, Pallas kernels, solve_step(): pl.pallas_call(functools.partial(solve_kernel, nodes), out_shape=(jax.Sha...  16.4 us
    pallas_call x1, Pallas kernels, densify(): pl.pallas_call(functools.partial(densify_kernel, RT, pair), out_shape=(de...  13.5 us

profile of v3, /device:TPU:0, one launch (start us, length us, event | category | flops | bytes accessed | tf_op | source)
XLA Modules:
  0.0 110.0 jit_solution(17307352529540634841)
XLA Ops:
  1.3 13.5 %densify.1 = (bf16[8,1024,256]{2,1,0:T(8,128)(2,1)}, bf16[8,1024,256]{2,1,0:T(8,128)(2,1)}) custom-call(s32[1,1,320]{2,1,0:T(1,128)} %rows_ref.1, s32[1,1,320]{2,1,0:T(1,128)} %cols_ref.1, s32[1,1]{1,0:T(1,128)S(6)} %copy.7.count_ref, bf16[320,128,128]{2,1,0:T(8,128)(2,1)} %bitcast.3), custom_call_target="tpu_custom_call" | custom-call | tf_op jit(solution)/shard_map/densify/pallas_call | solution.py:76
  14.8 39.5 %image_step.2 = (f32[160,256]{1,0:T(8,128)}, f32[192,128]{1,0:T(8,128)}) custom-call(bf16[160,256]{1,0:T(8,128)(2,1)} %bitcast.4, bf16[8,1024,256]{2,1,0:T(8,128)(2,1)} %get-tuple-element.11.high_hbm, bf16[8,1024,256]{2,1,0:T(8,128)(2,1)} %get-tuple-element.12.low_hbm), custom_call_target="tpu_custom_call" | custom-call | tf_op jit(solution)/shard_map/image_step/pallas_call | solution.py:234
  54.4 8.2 %solve_step.2 = (f32[160,256]{1,0:T(8,128)}, bf16[160,256]{1,0:T(8,128)(2,1)}, f32[160,160]{1,0:T(8,128)}) custom-call(f32[192,128]{1,0:T(8,128)} %get-tuple-element.13.packed_ref, f32[160,256]{1,0:T(8,128)} %get-tuple-element.14.image_ref), custom_call_target="tpu_custom_call" | custom-call | tf_op jit(solution)/shard_map/solve_step/pallas_call | solution.py:305
  62.6 39.3 %image_step.3 = (f32[160,256]{1,0:T(8,128)}, f32[192,128]{1,0:T(8,128)}) custom-call(bf16[160,256]{1,0:T(8,128)(2,1)} %get-tuple-element.15.current_ref, bf16[8,1024,256]{2,1,0:T(8,128)(2,1)} %get-tuple-element.11.high_hbm, bf16[8,1024,256]{2,1,0:T(8,128)(2,1)} %get-tuple-element.12.low_hbm), custom_call_target="tpu_custom_call" | custom-call | tf_op jit(solution)/shard_map/image_step/pallas_call | solution.py:234
  101.8 8.2 %solve_step.3 = (f32[160,256]{1,0:T(8,128)}, bf16[160,256]{1,0:T(8,128)(2,1)}, f32[160,160]{1,0:T(8,128)}) custom-call(f32[192,128]{1,0:T(8,128)} %get-tuple-element.16.packed_ref, f32[160,256]{1,0:T(8,128)} %get-tuple-element.17.image_ref), custom_call_target="tpu_custom_call" | custom-call | tf_op jit(solution)/shard_map/solve_step/pallas_call | solution.py:305
